TPU v7x, 32 devices: a 4x4x1 block of a 4x4x8 slice. The times are simulated.
32 devices in a mesh: dp: 1 (over z), etp: 4 (over y), ep: 8 (over x, core).
Axes of the slice: x: 4, y: 4, z: 1, core: 2. Of those that a mesh axis runs over, the one named last changes fastest.
The devices are a block of a 4x4x8 slice.
Arguments:
- hidden: bfloat16 [16384, 1024], P(('dp', 'ep'))
- expert_ids: int32 [16384, 8], P(('dp', 'ep'))
- gate_wts: float32 [16384, 8], P(('dp', 'ep'))
- slot_pos: int32 [16384, 8], P(('dp', 'ep'))
- w_gate: bfloat16 [32, 1024, 512], P('ep', None, 'etp')
- w_up: bfloat16 [32, 1024, 512], P('ep', None, 'etp')
- w_down: bfloat16 [32, 512, 1024], P('ep', 'etp')
Outputs:
- output: bfloat16 [16384, 1024], P(('dp', 'ep'))
All inputs are finite; a program needn't handle non-finite values.
Results may differ from a plain program's by a relative error of at most 0.001.
Values are sent between devices in bfloat16 or wider.
A program may use at most 768 MiB of HBM per device.

v0:
```python
import jax
import jax.numpy as jnp
from jax import lax
from jax.sharding import PartitionSpec as P


def solution(mesh):
    group = mesh.shape['ep']
    row_spec = P(('dp', 'ep'), None)
    col_spec = P('ep', None, 'etp')
    in_specs = (row_spec, row_spec, row_spec, row_spec, col_spec, col_spec, P('ep', 'etp', None))

    def device_step(hidden, expert_ids, gate_wts, slot_pos, w_gate, w_up, w_down):
        rows_dev, d_model = hidden.shape
        top_k = expert_ids.shape[1]
        local_experts = w_gate.shape[0]
        experts = local_experts * group
        local_cap = ((5 * top_k * rows_dev) // (4 * experts) + 7) // 8 * 8
        capacity = group * local_cap
        tokens = rows_dev * group
        n_slots = local_experts * capacity
        all_hidden = lax.all_gather(hidden, 'ep', axis=0, tiled=True)
        all_ids = lax.all_gather(expert_ids, 'ep', axis=0, tiled=True)
        all_gates = lax.all_gather(gate_wts, 'ep', axis=0, tiled=True)
        all_pos = lax.all_gather(slot_pos, 'ep', axis=0, tiled=True)
        local_ids = all_ids - lax.axis_index('ep') * local_experts
        is_kept = (all_pos >= 0) & (local_ids >= 0) & (local_ids < local_experts)
        slot_index = jnp.where(is_kept, local_ids * capacity + all_pos, n_slots).reshape(-1)
        token_index = jnp.broadcast_to(jnp.arange(tokens, dtype=jnp.int32)[:, None], (tokens, top_k)).reshape(-1)
        slot_token = jnp.full((n_slots,), tokens, jnp.int32).at[slot_index].set(token_index, mode='drop')
        slot_gate = jnp.zeros((n_slots,), jnp.float32).at[slot_index].set(all_gates.reshape(-1), mode='drop')
        buffer = jnp.take(all_hidden, slot_token, axis=0, mode='fill', fill_value=0).reshape(local_experts, capacity, d_model)
        h_gate = jnp.einsum('ecd,edf->ecf', buffer, w_gate, preferred_element_type=jnp.float32)
        h_up = jnp.einsum('ecd,edf->ecf', buffer, w_up, preferred_element_type=jnp.float32)
        hidden_act = (jax.nn.silu(h_gate) * h_up).astype(jnp.bfloat16)
        expert_out = jnp.einsum('ecf,efd->ecd', hidden_act, w_down, preferred_element_type=jnp.float32)
        weighted = expert_out.reshape(n_slots, d_model) * slot_gate[:, None]
        part_sum = jax.ops.segment_sum(weighted, slot_token, num_segments=tokens)
        own_rows = lax.psum_scatter(part_sum, 'ep', scatter_dimension=0, tiled=True)
        summed = lax.psum(own_rows, 'etp')
        return summed.astype(jnp.bfloat16)

    return jax.shard_map(device_step, mesh=mesh, in_specs=in_specs, out_specs=row_spec, check_vma=False)
```

profile of v0, /device:TPU:97, one launch (start us, length us, event | category | flops | bytes accessed | tf_op | source)
XLA Modules:
  0.0 2784.0 jit_solution(1321048565333421317)
XLA Ops:
  6.5 0.0 copy-start
  6.6 0.0 copy-start.2
  6.6 0.0 all-gather.2.cloned.1.call-start
  6.6 0.7 all-gather.2.cloned.1.call-update
  7.3 0.1 reduce-scatter.2.cloned.1.call-start
  7.4 19.6 all_gather.12
  27.0 27.2 all_gather.13
  54.1 0.2 add_select_fusion
  54.3 5.2 copy.8
  59.5 7.8 reshape.53
  67.3 3.5 broadcast_in_dim.42
  70.8 6.4 reshape.69
  77.1 0.5 compare_select_fusion
  77.7 478.7 %scatter_custom_fusion = s32[20480]{0:T(1024)S(1)} fusion(s32[131072]{0:T(1024)S(1)} %bitcast.12, s32[131072]{0:T(1024)S(1)} %reshape.69, s32[]{:T(128)} %constant.11.clone.1), kind=kCustom, calls=%fused_computation.25 | custom fusion | bytes 81924 | tf_op jit(solution)/shard_map/scatter | solution.py:30
  556.4 0.0 copy-done.2
  556.4 20.3 all_gather.15
  576.8 5.4 copy.9
  582.2 6.4 reshape.77
  588.6 11.3 sort
  599.9 488.3 %scatter_custom_fusion.1 = f32[20480]{0:T(1024)} fusion(s32[131072]{0:T(1024)S(1)} %bitcast.13, f32[131072]{0:T(1024)S(1)} %reshape.77, f32[]{:T(128)} %constant.10.clone.1), kind=kCustom, calls=%fused_computation.23 | custom fusion | bytes 81924 | tf_op jit(solution)/shard_map/scatter | solution.py:31
  1088.3 0.6 broadcast_clamp_fusion
  1088.9 666.2 %gather_fusion = bf16[20480,1024]{1,0:T(8,128)(2,1)} fusion(bf16[16384,1024]{1,0:T(8,128)(2,1)} %all-gather.2.cloned.1.call-done, s32[20480]{0:T(1024)S(1)} %fusion.12), kind=kCustom, calls=%fused_computation | custom fusion | bytes 83968000 | tf_op jit(solution)/shard_map/jit(_take)/gather | solution.py:32
  1755.1 0.0 copy-done.3
  1755.1 22.2 fusion.6
  1777.2 0.0 copy-done
  1777.2 49.9 %fusion.10 = f32[4,5120,1024]{2,1,0:T(8,128)} fusion(bf16[4,128,1024]{2,1,0:T(8,128)(2,1)S(1)} %copy-done, f32[4,5120,128]{2,1,0:T(8,128)} %fusion.6, bf16[4,1024,128]{2,1,0:T(8,128)(2,1)} %param.12, bf16[4,5120,1024]{2,1,0:T(8,128)(2,1)} %bitcast.11, pred[4,5120]{1,0:T(4,128)(4,1)S(1)} %broadcast_in_dim.44), kind=kOutput, calls=%fused_computation.15 | convolution fusion | flops 10774118400 | bytes 138432512 | tf_op jit(solution)/shard_map/ecf,efd->ecd/dot_general | solution.py:36
  1827.2 0.0 copy-done.1
  1827.2 54.5 %bitcast_multiply_fusion = f32[20480,1024]{1,0:T(8,128)} fusion(f32[4,5120,1024]{2,1,0:T(8,128)} %fusion.10, f32[20480]{0:T(1024)S(1)} %copy-done.1), kind=kLoop, calls=%fused_computation.7 | loop fusion | flops 20971520 | bytes 167854080 | tf_op jit(solution)/shard_map/mul | solution.py:37
  1881.6 369.7 %scatter_custom_fusion.2 = f32[16384,1024]{1,0:T(8,128)} fusion(s32[20480]{0:T(1024)} %get-tuple-element.5, f32[20480,1024]{1,0:T(8,128)} %bitcast_multiply_fusion, s32[20480]{0:T(1024)} %broadcast_clamp_fusion, f32[]{:T(128)} %constant.10.clone.1), kind=kCustom, calls=%fused_computation.5 | custom fusion | flops 20971520 | bytes 67109376 | tf_op jit(solution)/shard_map/scatter-add | solution.py:38
  2251.3 0.1 reduce-scatter.2.cloned.1.call-update
  2251.4 378.6 %reduce-scatter.2.cloned.1.call-done = f32[2048,1024]{1,0:T(8,128)} async-done(((f32[16384,1024]{1,0:T(8,128)}), f32[2048,1024]{1,0:T(8,128)}) %reduce-scatter.2.cloned.1.call-update) | async-done | bytes 8388624 | tf_op jit(solution)/shard_map/reduce_scatter | solution.py:39
  2630.0 146.8 %all-reduce.1 = bf16[2048,1024]{1,0:T(8,128)(2,1)} all-reduce(f32[2048,1024]{1,0:T(8,128)} %reduce-scatter.2.cloned.1.call-done), channel_id=1, replica_groups=mesh['dp'=1,'etp'=4,'ep'=8] {'etp'}, use_global_device_ids=true, to_apply=%region_4.5 | all-reduce | flops 2097152 | bytes 12582912 | tf_op jit(solution)/shard_map/psum | solution.py:40
  (7 shorter events, 0.1 us)
Async XLA Ops:
  6.5 1770.7 %copy-start = (bf16[4,128,1024]{2,1,0:T(8,128)(2,1)S(1)}, bf16[4,128,1024]{2,1,0:T(8,128)(2,1)}, u32[]{:S(2)}) copy-start(bf16[4,128,1024]{2,1,0:T(8,128)(2,1)} %param.13) | copy-start | bytes 3145732
  6.6 549.9 %copy-start.2 = (f32[2048,8]{0,1:T(8,128)S(1)}, f32[2048,8]{0,1:T(8,128)}, u32[]{:S(2)}) copy-start(f32[2048,8]{0,1:T(8,128)} %param.9) | copy-start | bytes 196612
  6.6 1082.3 %all-gather.2.cloned.1.call-start = ((), (), s32[]{:S(2)}) async-start(), calls=%async_computation.1 | async-start | bytes 37748736 | tf_op jit(solution)/shard_map/all_gather | solution.py:22
  7.3 2622.7 %reduce-scatter.2.cloned.1.call-start = ((), (), s32[]{:S(2)}) async-start(), calls=%async_computation.2 | async-start | bytes 75497472 | tf_op jit(solution)/shard_map/reduce_scatter | solution.py:39
  1088.9 666.2 %copy-start.3 = (bf16[4,1024,128]{2,1,0:T(8,128)(2,1)S(1)}, bf16[4,1024,128]{2,1,0:T(8,128)(2,1)}, u32[]{:S(2)}) copy-start(bf16[4,1024,128]{2,1,0:T(8,128)(2,1)} %param.11) | copy-start | bytes 3145732
  1777.2 49.9 %copy-start.1 = (f32[20480]{0:T(1024)S(1)}, f32[20480]{0:T(1024)}, u32[]{:S(2)}) copy-start(f32[20480]{0:T(1024)} %scatter_custom_fusion.1) | copy-start | bytes 245764
Sparse Core Ops, SparseCore 0:
  9.0 162.0 all-gather.1
  2251.5 378.4 reduce-scatter.1
where the time goes:
time: 2840 us; the launch traced here: 2780 us
  local copies, waits for them, and re-layouts  1670 us (59%)
  other arithmetic  437 us (15%)
  waiting for transfers between devices  379 us (13%)
  blocking collectives  214 us (8%)
  matrix products  72.1 us (3%)
    gather x1, local copies, waits for them, and re-layouts, device_step(): jnp.take(all_hidden, slot_token, axis=0, mode='fill', fill_value=0)  666 us
    scatter x1, local copies, waits for them, and re-layouts, device_step(): jnp.zeros((n_slots,), jnp.float32).at[slot_index]  488 us
    scatter x1, local copies, waits for them, and re-layouts, device_step(): jnp.full((n_slots,), tokens, jnp.int32).at[slot_index]  479 us
    scatter-add x3, other arithmetic, device_step(): part_sum = jax.ops.segment_sum(weighted, slot_token, num_segments=tokens)  382 us
    reduce_scatter x1, waiting for transfers between devices, device_step(): own_rows = lax.psum_scatter(part_sum, 'ep', scatter_dimension=0, tiled=True)  379 us
    psum x1, blocking collectives, device_step(): summed = lax.psum(own_rows, 'etp')  147 us
  transfers between devices with their start and end apart: 2, of which 1 were waited for; matrix products, arithmetic and copies ran while one was open for 36% of the time, Pallas kernels for 0%

commit v1 on v0

v1 whole, which is shorter than its diff:
```python
import functools

import jax
import jax.numpy as jnp
from jax import lax
from jax.experimental import pallas as pl
from jax.experimental.pallas import tpu as pltpu
from jax.sharding import PartitionSpec as P


def experts_kernel(tok_ref, gate_ref, wgu_ref, wdn_ref, out_ref, act_ref):
    n_q, n_e, d_model, two_f = wgu_ref.shape
    half = two_f // 2
    for e in range(n_e):
        gate = gate_ref[:, e:e + 1]
        for q in range(n_q):
            gu = jnp.dot(tok_ref[...], wgu_ref[q, e], preferred_element_type=jnp.float32)
            h_gate = gu[:, :half]
            act = jnp.where(gate > 0, jax.nn.silu(h_gate) * gu[:, half:], 0.0)
            act_ref[:, q * half:(q + 1) * half] = act.astype(jnp.bfloat16)
        down = wdn_ref[:, e].reshape(n_q * half, d_model)
        term = gate * jnp.dot(act_ref[...], down, preferred_element_type=jnp.float32)
        if e == 0:
            out_ref[...] = term
        else:
            out_ref[...] += term


def solution(mesh):
    row_spec = P(('dp', 'ep'), None)
    col_spec = P('ep', None, 'etp')
    in_specs = (row_spec, row_spec, row_spec, row_spec, col_spec, col_spec, P('ep', 'etp', None))
    n_q = mesh.shape['etp']
    group = mesh.shape['ep']

    def device_step(hidden, expert_ids, gate_wts, slot_pos, w_gate, w_up, w_down):
        rows_dev, d_model = hidden.shape
        n_e = w_gate.shape[0]
        width = w_gate.shape[2]
        rows = rows_dev // n_q
        start = lax.axis_index('etp') * rows
        cut = lambda a: lax.dynamic_slice_in_dim(a, start, rows, axis=0)
        ids, gts, pos = cut(expert_ids), cut(gate_wts), cut(slot_pos)
        hit = (ids[:, :, None] == jnp.arange(n_e * group, dtype=jnp.int32)[None, None, :]) & (pos >= 0)[:, :, None]
        dense = jnp.sum(jnp.where(hit, gts[:, :, None], 0.0), axis=1)
        all_gates = lax.all_gather(dense, 'ep', axis=0, tiled=True)
        gates = lax.dynamic_slice_in_dim(all_gates, lax.axis_index('ep') * n_e, n_e, axis=1)
        tok = lax.all_gather(cut(hidden), 'ep', axis=0, tiled=True)
        wgu = lax.all_gather(jnp.concatenate([w_gate, w_up], axis=-1), 'etp')
        wdn = lax.all_gather(w_down, 'etp')
        n_tok = rows * group
        part = pl.pallas_call(
            experts_kernel,
            out_shape=jax.ShapeDtypeStruct((n_tok, d_model), jnp.float32),
            grid=(group,),
            in_specs=[
                pl.BlockSpec((rows, d_model), lambda i: (i, 0)),
                pl.BlockSpec((rows, n_e), lambda i: (i, 0)),
                pl.BlockSpec((n_q, n_e, d_model, 2 * width), lambda i: (0, 0, 0, 0)),
                pl.BlockSpec((n_q, n_e, width, d_model), lambda i: (0, 0, 0, 0)),
            ],
            out_specs=pl.BlockSpec((rows, d_model), lambda i: (i, 0)),
            scratch_shapes=[pltpu.VMEM((rows, n_q * width), jnp.bfloat16)],
            compiler_params=pltpu.CompilerParams(vmem_limit_bytes=60 * 1024 * 1024),
            cost_estimate=pl.CostEstimate(flops=6 * n_tok * n_e * d_model * n_q * width, bytes_accessed=8 * n_tok * d_model, transcendentals=0),
        )(tok, gates, wgu, wdn)
        own = lax.psum_scatter(part, 'ep', scatter_dimension=0, tiled=True)
        return lax.all_gather(own.astype(jnp.bfloat16), 'etp', axis=0, tiled=True)

    return jax.shard_map(device_step, mesh=mesh, in_specs=in_specs, out_specs=row_spec, check_vma=False)
```

time: 2840 us -> 400 us (0.14); the launches traced: 2780 us -> 400 us
  local copies, waits for them, and re-layouts: 1670 us -> 9.71 us
  other arithmetic: 437 us -> 6.67 us
  blocking collectives: 214 us -> 25.2 us
  waiting for transfers between devices: 379 us -> 285 us
  matrix products: 72.1 us -> 0 us
  Pallas kernels: 0 us -> 60.2 us
    scatter x2 -> x0, local copies, waits for them, and re-layouts: 967 us -> none  [the longest x1 488 us: device_step(): jnp.zeros((n_slots,), jnp.float32).at[slot_index]]
    gather x1 -> x0, local copies, waits for them, and re-layouts: 666 us -> none  [device_step(): jnp.take(all_hidden, slot_token, axis=0, mode='fill', fill_value=0)]
    scatter-add x3 -> x0, other arithmetic: 382 us -> none  [device_step(): part_sum = jax.ops.segment_sum(weighted, slot_token, num_segments=tokens)]
    reduce_scatter x1, waiting for transfers between devices: 379 us -> 88.8 us  [device_step(): own = lax.psum_scatter(part, 'ep', scatter_dimension=0, tiled=True)]
    all_gather x1 -> x4, waiting for transfers between devices: 0.01 us -> 195 us  [the longest x1 82.8 us: device_step(): wgu = lax.all_gather(jnp.concatenate([w_gate, w_up], axis=-1), 'etp')]
    psum x1 -> x0, blocking collectives: 147 us -> none  [device_step(): summed = lax.psum(own_rows, 'etp')]
    dot_general x2 -> x0, matrix products: 72.1 us -> none  [the longest x1 49.9 us: device_step(): jnp.einsum('ecf,efd->ecd', hidden_act, w_down, preferred_element_type=jnp...]
    pallas_call x0 -> x1, Pallas kernels: none -> 60.2 us  [device_step(): pl.pallas_call(experts_kernel, out_shape=jax.ShapeDtypeStruct((n_tok, d_m...]
  transfers between devices with their start and end apart: 2 -> 5, of which waited for: 1 -> 5; matrix products, arithmetic and copies ran while one was open for 36% -> 2% of each run, Pallas kernels for 0% -> 0%
where the time goes in v1:
time: 400 us
  waiting for transfers between devices  285 us (71%)
  Pallas kernels  60.2 us (15%)
  blocking collectives  25.2 us (6%)
  between operations  13.2 us (3%)
  local copies, waits for them, and re-layouts  9.71 us (2%)
  other arithmetic  6.67 us (2%)
    reduce_scatter x1, waiting for transfers between devices, device_step(): own = lax.psum_scatter(part, 'ep', scatter_dimension=0, tiled=True)  88.8 us
    all_gather x1, waiting for transfers between devices, device_step(): wgu = lax.all_gather(jnp.concatenate([w_gate, w_up], axis=-1), 'etp')  82.8 us
    pallas_call x1, Pallas kernels, device_step(): pl.pallas_call(experts_kernel, out_shape=jax.ShapeDtypeStruct((n_tok, d_m...  60.2 us
    all_gather x1, waiting for transfers between devices, device_step(): tok = lax.all_gather(cut(hidden), 'ep', axis=0, tiled=True)  50.1 us
    all_gather x1, waiting for transfers between devices, device_step(): return lax.all_gather(own.astype(jnp.bfloat16), 'etp', axis=0, tiled=True)  45.6 us
    all_gather x1, blocking collectives, device_step(): all_gates = lax.all_gather(dense, 'ep', axis=0, tiled=True)  25.2 us
    all_gather x1, waiting for transfers between devices, device_step(): wdn = lax.all_gather(w_down, 'etp')  16.3 us
  transfers between devices with their start and end apart: 5, of which 5 were waited for; matrix products, arithmetic and copies ran while one was open for 2% of the time, Pallas kernels for 0%

profile of v1, /device:TPU:97, one launch (start us, length us, event | category | flops | bytes accessed | tf_op | source)
XLA Modules:
  0.0 399.7 jit_solution(2117553354306773813)
XLA Ops:
  6.5 0.0 copy-start
  6.6 0.0 all-gather.13.cloned.1.call-start
  6.6 0.7 all-gather.13.cloned.1.call-update
  7.3 0.1 all-gather.11.cloned.1.call-start
  7.4 3.1 pad_maximum_fusion
  10.5 0.1 all-gather.11.cloned.1.call-update
  10.5 0.1 all-gather.7.cloned.1.call-start
  10.6 2.3 constant_dynamic-slice_fusion.3
  12.9 0.1 all-gather.7.cloned.1.call-update
  13.0 0.1 reduce-scatter.2.cloned.1.call-start
  13.0 0.7 dynamic-slice_compare_fusion
  13.8 0.0 copy-done
  13.8 0.7 constant_dynamic-slice_fusion
  14.5 0.1 select_reduce_fusion
  14.6 0.1 copy.14
  14.8 25.2 %all_gather.22 = f32[4096,32]{1,0:T(8,128)S(1)} all-gather(f32[512,32]{1,0:T(8,128)S(1)} %copy.14), channel_id=1, replica_groups=mesh['dp'=1,'etp'=4,'ep'=8] {'ep'}, dimensions={0}, use_global_device_ids=true | all-gather | bytes 589824 | tf_op jit(solution)/shard_map/all_gather | solution.py:46
  39.9 1.9 constant_dynamic-slice_fusion.1.gate_ref
  41.9 16.3 %all-gather.13.cloned.1.call-done = bf16[16,128,1024]{2,1,0:T(8,128)(2,1)} async-done(((bf16[4,128,1024]{2,1,0:T(8,128)(2,1)}), bf16[16,128,1024]{2,1,0:T(8,128)(2,1)}) %all-gather.13.cloned.1.call-update) | async-done | bytes 4194320 | tf_op jit(solution)/shard_map/all_gather | solution.py:50
  58.2 82.8 %all-gather.11.cloned.1.call-done = bf16[16,1024,256]{2,1,0:T(8,128)(2,1)} async-done(((bf16[4,1024,256]{2,1,0:T(8,128)(2,1)}), bf16[16,1024,256]{2,1,0:T(8,128)(2,1)}) %all-gather.11.cloned.1.call-update) | async-done | bytes 8388624 | tf_op jit(solution)/shard_map/all_gather | solution.py:49
  141.0 50.1 %all-gather.7.cloned.1.call-done.tok_ref = bf16[4096,1024]{1,0:T(8,128)(2,1)} async-done(((bf16[512,1024]{1,0:T(8,128)(2,1)}), bf16[4096,1024]{1,0:T(8,128)(2,1)}) %all-gather.7.cloned.1.call-update) | async-done | bytes 8388624 | tf_op jit(solution)/shard_map/all_gather | solution.py:48
  191.1 60.2 %shard_map.73 = f32[4096,1024]{1,0:T(8,128)} custom-call(bf16[4096,1024]{1,0:T(8,128)(2,1)} %all-gather.7.cloned.1.call-done.tok_ref, f32[4096,4]{1,0:T(8,128)} %constant_dynamic-slice_fusion.1.gate_ref, bf16[4,4,1024,256]{3,2,1,0:T(8,128)(2,1)} %bitcast.2, bf16[4,4,128,1024]{3,2,1,0:T(8,128)(2,1)} %bitcast.3), custom_call_target="tpu_custom_call" | custom-call | flops 51539607552 | bytes 33554432 | tf_op jit(solution)/shard_map/pallas_call | solution.py:52
  251.3 0.1 reduce-scatter.2.cloned.1.call-update
  251.4 0.1 all-gather.9.cloned.1.call-start
  251.4 88.8 %reduce-scatter.2.cloned.1.call-done = f32[512,1024]{1,0:T(8,128)} async-done(((f32[4096,1024]{1,0:T(8,128)}), f32[512,1024]{1,0:T(8,128)}) %reduce-scatter.2.cloned.1.call-update) | async-done | bytes 2097168 | tf_op jit(solution)/shard_map/reduce_scatter | solution.py:67
  340.2 2.7 convert_element_type.3
  342.9 0.1 all-gather.9.cloned.1.call-update
  343.0 45.6 %all-gather.9.cloned.1.call-done = bf16[2048,1024]{1,0:T(8,128)(2,1)} async-done(((bf16[512,1024]{1,0:T(8,128)(2,1)}), bf16[2048,1024]{1,0:T(8,128)(2,1)}) %all-gather.9.cloned.1.call-update) | async-done | bytes 4194320 | tf_op jit(solution)/shard_map/all_gather | solution.py:68
  388.6 4.6 %copy.16 = bf16[2048,1024]{1,0:T(8,128)(2,1)} copy(bf16[2048,1024]{1,0:T(8,128)(2,1)} %all-gather.9.cloned.1.call-done) | data formatting | bytes 8388608
  (1 shorter events, 0.0 us)
Async XLA Ops:
  6.5 7.2 %copy-start = (s32[2048,8]{0,1:T(8,128)S(1)}, s32[2048,8]{0,1:T(8,128)}, u32[]{:S(2)}) copy-start(s32[2048,8]{0,1:T(8,128)} %param.8) | copy-start | bytes 196612
  6.6 51.6 %all-gather.13.cloned.1.call-start = ((), (), s32[]{:S(2)}) async-start(), calls=%async_computation.5 | async-start | bytes 5242880 | tf_op jit(solution)/shard_map/all_gather | solution.py:50
  7.3 133.7 %all-gather.11.cloned.1.call-start = ((), (), s32[]{:S(2)}) async-start(), calls=%async_computation.4 | async-start | bytes 10485760 | tf_op jit(solution)/shard_map/all_gather | solution.py:49
  10.5 180.6 %all-gather.7.cloned.1.call-start = ((), (), s32[]{:S(2)}) async-start(), calls=%async_computation.1 | async-start | bytes 9437184 | tf_op jit(solution)/shard_map/all_gather | solution.py:48
  13.0 327.2 %reduce-scatter.2.cloned.1.call-start = ((), (), s32[]{:S(2)}) async-start(), calls=%async_computation.2 | async-start | bytes 18874368 | tf_op jit(solution)/shard_map/reduce_scatter | solution.py:67
  251.4 137.2 %all-gather.9.cloned.1.call-start = ((), (), s32[]{:S(2)}) async-start(), calls=%async_computation.3 | async-start | bytes 5242880 | tf_op jit(solution)/shard_map/all_gather | solution.py:68
Sparse Core Ops, SparseCore 0:
  8.9 49.2 all-gather.12
  59.7 81.1 all-gather.10
  142.6 48.4 all-gather.6
  251.5 88.6 reduce-scatter.1
  343.1 45.4 all-gather.8

commit v2 on v0

v2 whole, which is shorter than its diff:
```python
import functools

import jax
import jax.numpy as jnp
from jax import lax
from jax.experimental import pallas as pl
from jax.experimental.pallas import tpu as pltpu
from jax.sharding import PartitionSpec as P

MESH = pl.DeviceIdType.MESH
CHUNKS = 4


def moe_kernel(n_q, group, hid, gat, wg, wu, wd, out, tok, gts, wgu, wdn, act, spart, pr, acc, r1, r2, fin, ssem, rsem, lsem, credit):
    rows, d_model = tok.shape[1:]
    n_e, width = wg.shape[0], wg.shape[2]
    cw = d_model // CHUNKS
    nx = group // 2
    hr, hk, he = rows // 2, d_model // 2, n_e // 2
    q, ep = lax.axis_index('etp'), lax.axis_index('ep')
    x, c = lax.div(ep, 2), lax.rem(ep, 2)
    yl, yr = lax.rem(q + n_q - 1, n_q), lax.rem(q + 1, n_q)
    xl, xr, xf = lax.rem(x + nx - 1, nx), lax.rem(x + 1, nx), lax.rem(x + 2, nx)
    bl, br, bf = xl * 2 + c, xr * 2 + c, xf * 2 + c
    to_l, to_r, to_p = {'ep': bl}, {'ep': br}, {'ep': x * 2 + 1 - c}
    up_l, up_r = {'etp': yl}, {'etp': yr}
    used = [0, 0]
    sends, locals_ = [], []

    def remote(src, dst, dev):
        k = used[0]
        used[0] += 1
        cp = pltpu.make_async_remote_copy(src_ref=src, dst_ref=dst, send_sem=ssem.at[k], recv_sem=rsem.at[k], device_id=dev, device_id_type=MESH)
        cp.start()
        sends.append(cp)
        return cp

    def local(src, dst):
        k = used[1]
        used[1] += 1
        cp = pltpu.make_async_copy(src, dst, lsem.at[k])
        cp.start()
        return cp

    barrier = pltpu.get_barrier_semaphore()
    for dev in (to_l, to_r, to_p, up_l, up_r):
        pl.semaphore_signal(barrier, inc=1, device_id=dev, device_id_type=MESH)
    pl.semaphore_wait(barrier, 5)

    def send_gu(e):
        cps = []
        for dev in (up_r, up_l):
            cps.append(remote(wg.at[e], wgu.at[e, q, :, 0:width], dev))
            cps.append(remote(wu.at[e], wgu.at[e, q, :, width:2 * width], dev))
        return cps

    def pass_gu(e, cps):
        for cp in cps:
            cp.wait_recv()
        return [
            remote(wgu.at[e, yl, 0:hk], wgu.at[e, yl, 0:hk], up_r),
            remote(wgu.at[e, yr, hk:d_model], wgu.at[e, yr, hk:d_model], up_l),
        ]

    def send_dn(n):
        return [remote(wd.at[:, :, n * cw:(n + 1) * cw], wdn.at[n, :, q], dev) for dev in (up_r, up_l)]

    def pass_dn(n, cps):
        for cp in cps:
            cp.wait_recv()
        return [
            remote(wdn.at[n, 0:he, yl], wdn.at[n, 0:he, yl], up_r),
            remote(wdn.at[n, he:n_e, yr], wdn.at[n, he:n_e, yr], up_l),
        ]

    def arrive(cps):
        for cp in cps:
            cp.wait_recv()

    own_rows = hid.at[pl.ds(pl.multiple_of(q * rows, rows), rows)]
    gu = {0: send_gu(0)}
    tok_p = [remote(own_rows, tok.at[ep], to_p), remote(gat, gts.at[ep], to_p)]
    tok_r = [remote(own_rows, tok.at[ep], to_r), remote(gat, gts.at[ep], to_r)]
    tok_l = [remote(own_rows, tok.at[ep], to_l), remote(gat, gts.at[ep], to_l)]
    gu[1] = send_gu(1)
    mine = [local(own_rows, tok.at[ep]), local(gat, gts.at[ep])]
    for e in range(n_e):
        mine.append(local(wg.at[e], wgu.at[e, q, :, 0:width]))
        mine.append(local(wu.at[e], wgu.at[e, q, :, width:2 * width]))
    for n in range(CHUNKS):
        mine.append(local(wd.at[:, :, n * cw:(n + 1) * cw], wdn.at[n, :, q]))

    fwd, dn, fdn = {}, {}, {}
    fwd[0] = pass_gu(0, gu[0])
    gu[2] = send_gu(2)
    arrive(tok_r)
    arrive(tok_l)
    far = [
        remote(tok.at[bl, 0:hr], tok.at[bl, 0:hr], to_r),
        remote(gts.at[bl], gts.at[bl], to_r),
        remote(tok.at[br, hr:rows], tok.at[br, hr:rows], to_l),
    ]
    relay = [remote(tok.at[b], tok.at[b], to_p) for b in (bl, br)]
    relay += [remote(gts.at[b], gts.at[b], to_p) for b in (bl, br)]
    fwd[1] = pass_gu(1, gu[1])
    gu[3] = send_gu(3)
    arrive(far)
    relay += [remote(tok.at[bf], tok.at[bf], to_p), remote(gts.at[bf], gts.at[bf], to_p)]
    fwd[2] = pass_gu(2, gu[2])
    dn[0] = send_dn(0)
    for cp in mine:
        cp.wait()
    arrive(tok_p)
    arrive(relay)

    def gates_of(b):
        return gts[b, ep].T

    def up_phase(e):
        arrive(fwd[e])

        def body(b, carry):
            gate = gates_of(b)[:, e:e + 1]
            for j in range(n_q):
                prod = jnp.dot(tok[b], wgu[e, j], preferred_element_type=jnp.float32)
                h = jnp.where(gate > 0, jax.nn.silu(prod[:, :width]) * prod[:, width:], 0.0)
                act[b * n_e + e, :, j * width:(j + 1) * width] = h.astype(jnp.bfloat16)
            return carry

        lax.fori_loop(0, group, body, 0)

    up_phase(0)
    up_phase(1)
    fwd[3] = pass_gu(3, gu[3])
    dn[1] = send_dn(1)
    up_phase(2)
    fdn[0] = pass_dn(0, dn[0])
    dn[2] = send_dn(2)
    up_phase(3)
    fdn[1] = pass_dn(1, dn[1])
    dn[3] = send_dn(3)

    def down(n, b, dst):
        gate = gates_of(b)
        for e in range(n_e):
            mat = wdn[n, e].reshape(n_q * width, cw)
            term = gate[:, e:e + 1] * jnp.dot(act[b * n_e + e], mat, preferred_element_type=jnp.float32)
            if e == 0:
                dst[...] = term
            else:
                dst[...] += term

    d2d, first, second, outs, fouts = {}, {}, {}, {}, {}

    def phase_a(n):
        arrive(fdn[n])
        if n >= 1:
            d2d[n - 1].wait_send()
            sends[:] = [cp for cp in sends if cp is not d2d[n - 1]]

        def other(i, carry):
            xi = lax.rem(xf + i, nx)
            down(n, xi * 2 + 1 - c, spart.at[xi])
            return carry

        lax.fori_loop(0, nx, other, 0)
        if n >= 2:
            pl.semaphore_wait(credit.at[n % 2], 1)
        d2d[n] = remote(spart, pr.at[n % 2], to_p)

        def own(i, carry):
            xi = lax.rem(xf + i, nx)
            down(n, xi * 2 + c, acc.at[n, xi])
            return carry

        lax.fori_loop(0, nx, own, 0)

    def phase_b(n):
        d2d[n].wait_recv()
        acc[n, xf] += pr[n % 2, xf]
        first[n] = [
            remote(acc.at[n, xf, 0:hr], r1.at[n, 0], to_r),
            remote(acc.at[n, xf, hr:rows], r1.at[n, 1], to_l),
        ]
        acc[n, xr] += pr[n % 2, xr]
        acc[n, xl] += pr[n % 2, xl]
        second[n] = [
            remote(acc.at[n, xr, hr:rows], r2.at[n, 0, hr:rows], to_r),
            remote(acc.at[n, xl, 0:hr], r2.at[n, 1, 0:hr], to_l),
        ]
        acc[n, x] += pr[n % 2, x]
        if n + 2 < CHUNKS:
            pl.semaphore_signal(credit.at[n % 2], inc=1, device_id=to_p, device_id_type=MESH)

    def phase_c(n):
        first[n][0].wait_recv()
        acc[n, xr, 0:hr] += r1[n, 0]
        second[n].append(remote(acc.at[n, xr, 0:hr], r2.at[n, 0, 0:hr], to_r))
        first[n][1].wait_recv()
        acc[n, xl, hr:rows] += r1[n, 1]
        second[n].append(remote(acc.at[n, xl, hr:rows], r2.at[n, 1, hr:rows], to_l))

    def place(n, quarter, lo, hi):
        return out.at[pl.ds(pl.multiple_of(quarter * rows + lo, hr), hi - lo), n * cw:(n + 1) * cw]

    def phase_d(n):
        arrive(second[n])
        fin[n] = (acc[n, x] + r2[n, 0] + r2[n, 1]).astype(jnp.bfloat16)
        outs[n] = [remote(fin.at[n], place(n, q, 0, rows), dev) for dev in (up_r, up_l)]
        locals_.append(local(fin.at[n], place(n, q, 0, rows)))

    def phase_e(n):
        arrive(outs[n])
        fouts[n] = [
            remote(place(n, yl, 0, hr), place(n, yl, 0, hr), up_r),
            remote(place(n, yr, hr, rows), place(n, yr, hr, rows), up_l),
        ]

    phase_a(0)
    phase_b(0)
    fdn[2] = pass_dn(2, dn[2])
    phase_a(1)
    phase_b(1)
    phase_c(0)
    fdn[3] = pass_dn(3, dn[3])
    phase_a(2)
    phase_b(2)
    phase_c(1)
    phase_d(0)
    phase_a(3)
    phase_b(3)
    phase_c(2)
    phase_d(1)
    phase_e(0)
    phase_c(3)
    phase_d(2)
    phase_e(1)
    phase_d(3)
    phase_e(2)
    phase_e(3)
    for n in range(CHUNKS):
        arrive(fouts[n])
    for cp in sends:
        cp.wait_send()
    for cp in locals_:
        cp.wait()


def solution(mesh):
    row_spec = P(('dp', 'ep'), None)
    col_spec = P('ep', None, 'etp')
    in_specs = (row_spec, row_spec, row_spec, row_spec, col_spec, col_spec, P('ep', 'etp', None))
    n_q = mesh.shape['etp']
    group = mesh.shape['ep']

    def device_step(hidden, expert_ids, gate_wts, slot_pos, w_gate, w_up, w_down):
        rows_dev, d_model = hidden.shape
        n_e, _, width = w_gate.shape
        rows = rows_dev // n_q
        cw = d_model // CHUNKS
        nx = group // 2
        start = lax.axis_index('etp') * rows
        cut = lambda a: lax.dynamic_slice_in_dim(a, start, rows, axis=0).T
        ids, gts, pos = cut(expert_ids), cut(gate_wts), cut(slot_pos)
        wanted = jnp.arange(group, dtype=jnp.int32)[:, None] * n_e + jnp.arange(8, dtype=jnp.int32)[None, :]
        wanted = jnp.where(jnp.arange(8)[None, :] < n_e, wanted, -1)
        hit = (ids[None, None] == wanted[:, :, None, None]) & (pos >= 0)[None, None]
        dense = jnp.sum(jnp.where(hit, gts[None, None], 0.0), axis=2)
        f32, bf16 = jnp.float32, jnp.bfloat16
        return pl.pallas_call(
            functools.partial(moe_kernel, n_q, group),
            out_shape=jax.ShapeDtypeStruct((rows_dev, d_model), bf16),
            in_specs=[pl.BlockSpec(memory_space=pl.ANY)] * 5,
            out_specs=pl.BlockSpec(memory_space=pl.ANY),
            scratch_shapes=[
                pltpu.VMEM((group, rows, d_model), bf16),
                pltpu.VMEM((group, group, 8, rows), f32),
                pltpu.VMEM((n_e, n_q, d_model, 2 * width), bf16),
                pltpu.VMEM((CHUNKS, n_e, n_q, width, cw), bf16),
                pltpu.VMEM((group * n_e, rows, n_q * width), bf16),
                pltpu.VMEM((nx, rows, cw), f32),
                pltpu.VMEM((2, nx, rows, cw), f32),
                pltpu.VMEM((CHUNKS, nx, rows, cw), f32),
                pltpu.VMEM((CHUNKS, 2, rows // 2, cw), f32),
                pltpu.VMEM((CHUNKS, 2, rows, cw), f32),
                pltpu.VMEM((CHUNKS, rows, cw), bf16),
                pltpu.SemaphoreType.DMA((104,)),
                pltpu.SemaphoreType.DMA((104,)),
                pltpu.SemaphoreType.DMA((20,)),
                pltpu.SemaphoreType.REGULAR((2,)),
            ],
            compiler_params=pltpu.CompilerParams(collective_id=0, has_side_effects=True, vmem_limit_bytes=67043328),
        )(hidden, dense, w_gate, w_up, w_down)

    return jax.shard_map(device_step, mesh=mesh, in_specs=in_specs, out_specs=row_spec, check_vma=False)
```

time: 2840 us -> 198 us (0.07); the launches traced: 2780 us -> 198 us
  local copies, waits for them, and re-layouts: 1670 us -> 6.08 us
  other arithmetic: 437 us -> 1.94 us
  waiting for transfers between devices: 379 us -> 0 us
  blocking collectives: 214 us -> 0 us
  Pallas kernels: 0 us -> 190 us
  matrix products: 72.1 us -> 0 us
    scatter x2 -> x0, local copies, waits for them, and re-layouts: 967 us -> none  [the longest x1 488 us: device_step(): jnp.zeros((n_slots,), jnp.float32).at[slot_index]]
    gather x1 -> x0, local copies, waits for them, and re-layouts: 666 us -> none  [device_step(): jnp.take(all_hidden, slot_token, axis=0, mode='fill', fill_value=0)]
    scatter-add x3 -> x0, other arithmetic: 382 us -> none  [device_step(): part_sum = jax.ops.segment_sum(weighted, slot_token, num_segments=tokens)]
    reduce_scatter x1 -> x0, waiting for transfers between devices: 379 us -> none  [device_step(): own_rows = lax.psum_scatter(part_sum, 'ep', scatter_dimension=0, tiled=True)]
    pallas_call x0 -> x1, Pallas kernels: none -> 190 us  [device_step(): pl.pallas_call(functools.partial(moe_kernel, n_q, group), out_shape=jax.S...]
    psum x1 -> x0, blocking collectives: 147 us -> none  [device_step(): summed = lax.psum(own_rows, 'etp')]
    dot_general x2 -> x0, matrix products: 72.1 us -> none  [the longest x1 49.9 us: device_step(): jnp.einsum('ecf,efd->ecd', hidden_act, w_down, preferred_element_type=jnp...]
    all_gather x3 -> x0, blocking collectives: 67.1 us -> none  [the longest x1 27.2 us: device_step(): all_ids = lax.all_gather(expert_ids, 'ep', axis=0, tiled=True)]
  transfers between devices with their start and end apart: 2 -> 0, of which waited for: 1 -> 0; matrix products, arithmetic and copies ran while one was open for 36% -> 0% of each run, Pallas kernels for 0% -> 0%
where the time goes in v2:
time: 198 us
  Pallas kernels  190 us (96%)
  local copies, waits for them, and re-layouts  6.08 us (3%)
    pallas_call x1, Pallas kernels, device_step(): pl.pallas_call(functools.partial(moe_kernel, n_q, group), out_shape=jax.S...  190 us
    unnamed x1, local copies, waits for them, and re-layouts  4.64 us

profile of v2, /device:TPU:97, one launch (start us, length us, event | category | flops | bytes accessed | tf_op | source)
XLA Modules:
  0.0 197.8 jit_solution(12452586281344920973)
XLA Ops:
  0.0 0.1 add_select_fusion
  0.1 0.7 fusion
  0.8 0.7 dynamic-slice_bitcast_fusion.1
  1.5 0.7 dynamic-slice_bitcast_fusion
  2.2 1.1 select_reduce_fusion.gat
  3.4 189.8 %shard_map.73 = bf16[2048,1024]{1,0:T(8,128)(2,1)} custom-call(bf16[2048,1024]{1,0:T(8,128)(2,1)} %hid.1, f32[8,8,512]{2,1,0:T(8,128)} %select_reduce_fusion.gat, bf16[4,1024,128]{2,1,0:T(8,128)(2,1)} %wg.1, bf16[4,1024,128]{2,1,0:T(8,128)(2,1)} %wu.1, bf16[4,128,1024]{2,1,0:T(8,128)(2,1)} %wd.1), custom_call_target="tpu_custom_call" | custom-call | tf_op jit(solution)/shard_map/pallas_call | solution.py:270
  193.1 4.6 %copy.9 = bf16[2048,1024]{1,0:T(8,128)(2,1)} copy(bf16[2048,1024]{1,0:T(8,128)(2,1)} %shard_map.73) | data formatting | bytes 8388608
  (2 shorter events, 0.0 us)

commit v3 on v2

v3 whole, which is shorter than its diff:
```python
import functools

import jax
import jax.numpy as jnp
from jax import lax
from jax.experimental import pallas as pl
from jax.experimental.pallas import tpu as pltpu
from jax.sharding import PartitionSpec as P

MESH = pl.DeviceIdType.MESH
EIGHTHS = (2, 2, 2, 1, 1)


def moe_kernel(n_q, group, hid, ids, gts, pos, wg, wu, wd, out, tok, ids_v, gts_v, pos_v, gcol, wgu, act, spart, pr, *rest):
    n_c = len(EIGHTHS)
    wdn, acc, r1, r2, fin = (rest[i * n_c:(i + 1) * n_c] for i in range(5))
    ssem, rsem, lsem, credit = rest[5 * n_c:]
    rows, d_model = tok.shape[1:]
    n_e, width = wg.shape[0], wg.shape[2]
    nx = group // 2
    hr, hk, he = rows // 2, d_model // 2, n_e // 2
    wide = [k * (d_model // 8) for k in EIGHTHS]
    cols = [slice(sum(wide[:n]), sum(wide[:n + 1])) for n in range(n_c)]
    q, ep = lax.axis_index('etp'), lax.axis_index('ep')
    x, c = lax.div(ep, 2), lax.rem(ep, 2)
    yl, yr = lax.rem(q + n_q - 1, n_q), lax.rem(q + 1, n_q)
    xl, xr, xf = lax.rem(x + nx - 1, nx), lax.rem(x + 1, nx), lax.rem(x + 2, nx)
    bl, br, bf = xl * 2 + c, xr * 2 + c, xf * 2 + c
    to_l, to_r, to_p = {'ep': bl}, {'ep': br}, {'ep': x * 2 + 1 - c}
    up_l, up_r = {'etp': yl}, {'etp': yr}
    used = [0, 0]
    sends, placed = [], []

    def remote(src, dst, dev):
        k = used[0]
        used[0] += 1
        cp = pltpu.make_async_remote_copy(src_ref=src, dst_ref=dst, send_sem=ssem.at[k], recv_sem=rsem.at[k], device_id=dev, device_id_type=MESH)
        cp.start()
        sends.append(cp)
        return cp

    def local(src, dst):
        k = used[1]
        used[1] += 1
        cp = pltpu.make_async_copy(src, dst, lsem.at[k])
        cp.start()
        return cp

    def arrive(cps):
        for cp in cps:
            cp.wait_recv()

    barrier = pltpu.get_barrier_semaphore()
    for dev in (to_l, to_r, to_p, up_l, up_r):
        pl.semaphore_signal(barrier, inc=1, device_id=dev, device_id_type=MESH)
    pl.semaphore_wait(barrier, 5)

    def send_gu(e):
        cps = []
        for slot, dev in ((1, up_r), (2, up_l)):
            cps.append(remote(wg.at[e], wgu.at[e, slot, :, 0:width], dev))
            cps.append(remote(wu.at[e], wgu.at[e, slot, :, width:2 * width], dev))
        return cps

    def pass_gu(e, cps):
        arrive(cps)
        return [
            remote(wgu.at[e, 1, 0:hk], wgu.at[e, 3, 0:hk], up_r),
            remote(wgu.at[e, 2, hk:d_model], wgu.at[e, 3, hk:d_model], up_l),
        ]

    def send_dn(n):
        return [remote(wd.at[:, :, cols[n]], wdn[n].at[:, slot], dev) for slot, dev in ((1, up_r), (2, up_l))]

    def pass_dn(n, cps):
        arrive(cps)
        return [
            remote(wdn[n].at[0:he, 1], wdn[n].at[0:he, 3], up_r),
            remote(wdn[n].at[he:n_e, 2], wdn[n].at[he:n_e, 3], up_l),
        ]

    start = pl.multiple_of(q * rows, rows)
    own_rows = hid.at[pl.ds(start, rows)]
    route = [(a.at[:, pl.ds(start, rows)], v) for a, v in ((ids, ids_v), (gts, gts_v), (pos, pos_v))]

    def send_tok(dev):
        return [remote(own_rows, tok.at[ep], dev)] + [remote(a, v.at[ep], dev) for a, v in route]

    def pass_route(b, dev):
        return [remote(v.at[b], v.at[b], dev) for v in (ids_v, gts_v, pos_v)]

    gu = {0: send_gu(0)}
    tok_p, tok_r, tok_l = send_tok(to_p), send_tok(to_r), send_tok(to_l)
    gu[1] = send_gu(1)
    mine = [local(own_rows, tok.at[ep])] + [local(a, v.at[ep]) for a, v in route]
    for e in range(n_e):
        mine.append(local(wg.at[e], wgu.at[e, 0, :, 0:width]))
        mine.append(local(wu.at[e], wgu.at[e, 0, :, width:2 * width]))
    for n in range(n_c):
        mine.append(local(wd.at[:, :, cols[n]], wdn[n].at[:, 0]))

    def block_at(o):
        h = lax.div(o, 2)
        xi = lax.rem(x + h + lax.div(h, 2) - 2 * lax.div(h, 3), nx)
        return xi * 2 + lax.rem(o, 2)

    def make_gates(lo, hi):
        def body(o, carry):
            b = block_at(o)
            weight = jnp.where(pos_v[b] >= 0, gts_v[b], 0.0)
            chosen = ids_v[b]
            line = lax.broadcasted_iota(jnp.int32, weight.shape, 0)
            table = jnp.zeros_like(weight)
            for e in range(n_e):
                one = jnp.sum(jnp.where(chosen == ep * n_e + e, weight, 0.0), axis=0, keepdims=True)
                table = jnp.where(line == e, one, table)
            gcol[b] = table.T
            return carry

        lax.fori_loop(lo, hi, body, 0)

    def up(e0, e1, slots, lo, hi):
        def body(t, carry):
            b = block_at(lo + lax.div(t, e1 - e0))
            e = e0 + lax.rem(t, e1 - e0)
            gate = gcol[b, :, e0:e0 + 1] if e1 - e0 == 1 else None
            if gate is None:
                lane = lax.broadcasted_iota(jnp.int32, gcol.shape[1:], 1)
                gate = jnp.sum(jnp.where(lane == e, gcol[b], 0.0), axis=1, keepdims=True)
            for s in slots:
                prod = jnp.dot(tok[b], wgu[e, s], preferred_element_type=jnp.float32)
                h = jnp.where(gate > 0, jax.nn.silu(prod[:, :width]) * prod[:, width:], 0.0)
                act[b * n_e + e, :, s * width:(s + 1) * width] = h.astype(jnp.bfloat16)
            return carry

        lax.fori_loop(0, (hi - lo) * (e1 - e0), body, 0)

    fwd, dn, fdn = {}, {}, {}
    for cp in mine:
        cp.wait()
    arrive(tok_p)
    make_gates(0, 2)
    up(0, n_e, (0,), 0, 2)
    fwd[0] = pass_gu(0, gu[0])
    gu[2] = send_gu(2)
    up(0, 1, (1, 2), 0, 2)
    fwd[1] = pass_gu(1, gu[1])
    gu[3] = send_gu(3)
    up(1, 2, (1, 2), 0, 2)
    arrive(tok_r)
    arrive(tok_l)
    relay = [remote(tok.at[b], tok.at[b], to_p) for b in (bl, br)]
    far = [
        remote(tok.at[bl, 0:hr], tok.at[bl, 0:hr], to_r),
        remote(tok.at[br, hr:rows], tok.at[br, hr:rows], to_l),
    ]
    relay += pass_route(bl, to_p) + pass_route(br, to_p)
    far += pass_route(bl, to_r)
    arrive(relay)
    make_gates(2, 6)
    up(0, n_e, (0,), 2, 6)
    up(0, 2, (1, 2), 2, 6)
    arrive(far)
    relay = [remote(tok.at[bf], tok.at[bf], to_p)] + pass_route(bf, to_p)
    arrive(fwd[0])
    up(0, 1, (3,), 0, 6)
    fwd[2] = pass_gu(2, gu[2])
    arrive(relay)
    make_gates(6, 8)
    up(0, n_e, (0,), 6, 8)
    up(0, 2, (1, 2), 6, 8)
    up(0, 1, (3,), 6, 8)
    up(2, 3, (1, 2), 0, 8)
    arrive(fwd[1])
    up(1, 2, (3,), 0, 8)
    fwd[3] = pass_gu(3, gu[3])
    dn[0] = send_dn(0)
    up(3, 4, (1, 2), 0, 8)
    arrive(fwd[2])
    up(2, 3, (3,), 0, 8)
    arrive(fwd[3])
    up(3, 4, (3,), 0, 8)

    def down(n, b, dst):
        for e in range(n_e):
            mat = wdn[n][e].reshape(n_q * width, wide[n])
            term = gcol[b, :, e:e + 1] * jnp.dot(act[b * n_e + e], mat, preferred_element_type=jnp.float32)
            if e == 0:
                dst[...] = term
            else:
                dst[...] += term

    d2d, first, second, outs, fouts = {}, {}, {}, {}, {}

    def phase_a(n):
        arrive(fdn[n])
        if n >= 1:
            d2d[n - 1].wait_send()
            sends[:] = [cp for cp in sends if cp is not d2d[n - 1]]
        half = spart.at[:, :, 0:wide[n]]

        def other(i, carry):
            xi = lax.rem(xf + i, nx)
            down(n, xi * 2 + 1 - c, half.at[xi])
            return carry

        lax.fori_loop(0, nx, other, 0)
        if n >= 2:
            pl.semaphore_wait(credit.at[n % 2], 1)
        d2d[n] = remote(half, pr.at[n % 2, :, :, 0:wide[n]], to_p)

        def own(i, carry):
            xi = lax.rem(xf + i, nx)
            down(n, xi * 2 + c, acc[n].at[xi])
            return carry

        lax.fori_loop(0, nx, own, 0)

    def phase_b(n):
        d2d[n].wait_recv()

        def join(xi):
            acc[n][xi] += pr[n % 2, xi, :, 0:wide[n]]

        join(xf)
        first[n] = [
            remote(acc[n].at[xf, 0:hr], r1[n].at[0], to_r),
            remote(acc[n].at[xf, hr:rows], r1[n].at[1], to_l),
        ]
        join(xr)
        join(xl)
        second[n] = [
            remote(acc[n].at[xr, hr:rows], r2[n].at[0, hr:rows], to_r),
            remote(acc[n].at[xl, 0:hr], r2[n].at[1, 0:hr], to_l),
        ]
        join(x)
        if n + 2 < n_c:
            pl.semaphore_signal(credit.at[n % 2], inc=1, device_id=to_p, device_id_type=MESH)

    def phase_c(n):
        first[n][0].wait_recv()
        acc[n][xr, 0:hr] += r1[n][0]
        second[n].append(remote(acc[n].at[xr, 0:hr], r2[n].at[0, 0:hr], to_r))
        first[n][1].wait_recv()
        acc[n][xl, hr:rows] += r1[n][1]
        second[n].append(remote(acc[n].at[xl, hr:rows], r2[n].at[1, hr:rows], to_l))

    def place(n, quarter, lo, hi):
        return out.at[pl.ds(pl.multiple_of(quarter * rows + lo, hr), hi - lo), cols[n]]

    def phase_d(n):
        arrive(second[n])
        fin[n][...] = (acc[n][x] + r2[n][0] + r2[n][1]).astype(jnp.bfloat16)
        outs[n] = [remote(fin[n], place(n, q, 0, rows), dev) for dev in (up_r, up_l)]
        placed.append(local(fin[n], place(n, q, 0, rows)))

    def phase_e(n):
        arrive(outs[n])
        fouts[n] = [
            remote(place(n, yl, 0, hr), place(n, yl, 0, hr), up_r),
            remote(place(n, yr, hr, rows), place(n, yr, hr, rows), up_l),
        ]

    fdn[0] = pass_dn(0, dn[0])
    dn[1] = send_dn(1)
    dn[2] = send_dn(2)
    phase_a(0)
    phase_b(0)
    fdn[1] = pass_dn(1, dn[1])
    dn[3] = send_dn(3)
    dn[4] = send_dn(4)
    phase_c(0)
    phase_a(1)
    phase_b(1)
    fdn[2] = pass_dn(2, dn[2])
    phase_a(2)
    phase_b(2)
    fdn[3] = pass_dn(3, dn[3])
    phase_c(1)
    phase_d(0)
    phase_a(3)
    phase_b(3)
    fdn[4] = pass_dn(4, dn[4])
    phase_c(2)
    phase_d(1)
    phase_e(0)
    phase_a(4)
    phase_b(4)
    phase_c(3)
    phase_d(2)
    phase_e(1)
    phase_c(4)
    phase_d(3)
    phase_e(2)
    phase_d(4)
    phase_e(3)
    phase_e(4)
    for n in range(n_c):
        arrive(fouts[n])
    for cp in sends:
        cp.wait_send()
    for cp in placed:
        cp.wait()


def solution(mesh):
    row_spec = P(('dp', 'ep'), None)
    col_spec = P('ep', None, 'etp')
    in_specs = (row_spec, row_spec, row_spec, row_spec, col_spec, col_spec, P('ep', 'etp', None))
    n_q = mesh.shape['etp']
    group = mesh.shape['ep']

    def device_step(hidden, expert_ids, gate_wts, slot_pos, w_gate, w_up, w_down):
        rows_dev, d_model = hidden.shape
        top_k = expert_ids.shape[1]
        n_e, _, width = w_gate.shape
        rows = rows_dev // n_q
        nx = group // 2
        f32, bf16, i32 = jnp.float32, jnp.bfloat16, jnp.int32
        wide = [k * (d_model // 8) for k in EIGHTHS]
        chunked = [pltpu.VMEM((n_e, n_q, width, w), bf16) for w in wide]
        chunked += [pltpu.VMEM((nx, rows, w), f32) for w in wide]
        chunked += [pltpu.VMEM((2, rows // 2, w), f32) for w in wide]
        chunked += [pltpu.VMEM((2, rows, w), f32) for w in wide]
        chunked += [pltpu.VMEM((rows, w), bf16) for w in wide]
        return pl.pallas_call(
            functools.partial(moe_kernel, n_q, group),
            out_shape=jax.ShapeDtypeStruct((rows_dev, d_model), bf16),
            in_specs=[pl.BlockSpec(memory_space=pl.ANY)] * 7,
            out_specs=pl.BlockSpec(memory_space=pl.ANY),
            scratch_shapes=[
                pltpu.VMEM((group, rows, d_model), bf16),
                pltpu.VMEM((group, top_k, rows), i32),
                pltpu.VMEM((group, top_k, rows), f32),
                pltpu.VMEM((group, top_k, rows), i32),
                pltpu.VMEM((group, rows, top_k), f32),
                pltpu.VMEM((n_e, n_q, d_model, 2 * width), bf16),
                pltpu.VMEM((group * n_e, rows, n_q * width), bf16),
                pltpu.VMEM((nx, rows, max(wide)), f32),
                pltpu.VMEM((2, nx, rows, max(wide)), f32),
                *chunked,
                pltpu.SemaphoreType.DMA((132,)),
                pltpu.SemaphoreType.DMA((132,)),
                pltpu.SemaphoreType.DMA((24,)),
                pltpu.SemaphoreType.REGULAR((2,)),
            ],
            compiler_params=pltpu.CompilerParams(collective_id=0, has_side_effects=True, vmem_limit_bytes=67043328),
        )(hidden, expert_ids.T, gate_wts.T, slot_pos.T, w_gate, w_up, w_down)

    return jax.shard_map(device_step, mesh=mesh, in_specs=in_specs, out_specs=row_spec, check_vma=False)
```

time: 198 us -> 186 us (0.939)
  Pallas kernels: 190 us -> 182 us
    pallas_call x1, Pallas kernels: 190 us -> 182 us  [device_step(): pl.pallas_call(functools.partial(moe_kernel, n_q, group), out_shape=jax.S...]
where the time goes in v3:
time: 186 us
  Pallas kernels  182 us (98%)
  local copies, waits for them, and re-layouts  4.64 us (2%)
    pallas_call x1, Pallas kernels, device_step(): pl.pallas_call(functools.partial(moe_kernel, n_q, group), out_shape=jax.S...  182 us
    unnamed x1, local copies, waits for them, and re-layouts  4.64 us

profile of v3, /device:TPU:97, one launch (start us, length us, event | category | flops | bytes accessed | tf_op | source)
XLA Modules:
  0.0 186.2 jit_solution(1392566764599989491)
XLA Ops:
  0.0 181.5 %shard_map.73 = bf16[2048,1024]{1,0:T(8,128)(2,1)} custom-call(bf16[2048,1024]{1,0:T(8,128)(2,1)} %hid.1, s32[8,2048]{1,0:T(8,128)} %bitcast.3, f32[8,2048]{1,0:T(8,128)} %bitcast.4, s32[8,2048]{1,0:T(8,128)} %bitcast.5, bf16[4,1024,128]{2,1,0:T(8,128)(2,1)} %wg.1, bf16[4,1024,128]{2,1,0:T(8,128)(2,1)} %wu.1, bf16[4,128,1024]{2,1,0:T(8,128)(2,1)} %wd.1), custom_call_target="tpu_custom_call" | custom-call | tf_op jit(solution)/shard_map/pallas_call | solution.py:326
  181.5 4.6 %copy.9 = bf16[2048,1024]{1,0:T(8,128)(2,1)} copy(bf16[2048,1024]{1,0:T(8,128)(2,1)} %shard_map.73) | data formatting | bytes 8388608

commit v4 on v3

--- a/solution.py
+++ b/solution.py
@@ -8,17 +8,18 @@
 from jax.sharding import PartitionSpec as P
 
 MESH = pl.DeviceIdType.MESH
-EIGHTHS = (2, 2, 2, 1, 1)
+EIGHTHS = (1, 2, 2, 2, 1)
 
 
 def moe_kernel(n_q, group, hid, ids, gts, pos, wg, wu, wd, out, tok, ids_v, gts_v, pos_v, gcol, wgu, act, spart, pr, *rest):
     n_c = len(EIGHTHS)
-    wdn, acc, r1, r2, fin = (rest[i * n_c:(i + 1) * n_c] for i in range(5))
-    ssem, rsem, lsem, credit = rest[5 * n_c:]
+    wdn, acc, r1, r2 = (list(rest[i * n_c:(i + 1) * n_c]) for i in range(4))
+    ssem, rsem, lsem, credit = rest[4 * n_c:]
     rows, d_model = tok.shape[1:]
     n_e, width = wg.shape[0], wg.shape[2]
     nx = group // 2
     hr, hk, he = rows // 2, d_model // 2, n_e // 2
+    acc[n_c - 1] = acc[0]
     wide = [k * (d_model // 8) for k in EIGHTHS]
     cols = [slice(sum(wide[:n]), sum(wide[:n + 1])) for n in range(n_c)]
     q, ep = lax.axis_index('etp'), lax.axis_index('ep')
@@ -29,7 +30,7 @@
     to_l, to_r, to_p = {'ep': bl}, {'ep': br}, {'ep': x * 2 + 1 - c}
     up_l, up_r = {'etp': yl}, {'etp': yr}
     used = [0, 0]
-    sends, placed = [], []
+    sends = []
 
     def remote(src, dst, dev):
         k = used[0]
@@ -53,14 +54,25 @@
     barrier = pltpu.get_barrier_semaphore()
     for dev in (to_l, to_r, to_p, up_l, up_r):
         pl.semaphore_signal(barrier, inc=1, device_id=dev, device_id_type=MESH)
+
+    start = pl.multiple_of(q * rows, rows)
+    route = [(a.at[:, pl.ds(start, rows)], v) for a, v in ((ids, ids_v), (gts, gts_v), (pos, pos_v))]
+
+    def load_gu(e):
+        return [local(wg.at[e], wgu.at[e, 0, :, 0:width]), local(wu.at[e], wgu.at[e, 0, :, width:2 * width])]
+
+    mine_gu = {0: load_gu(0)}
+    mine_tok = [local(hid.at[pl.ds(start, rows)], tok.at[ep])] + [local(a, v.at[ep]) for a, v in route]
+    for e in range(1, n_e):
+        mine_gu[e] = load_gu(e)
+    mine_dn = [local(wd.at[:, :, cols[n]], wdn[n].at[:, 0]) for n in range(n_c)]
     pl.semaphore_wait(barrier, 5)
 
     def send_gu(e):
-        cps = []
-        for slot, dev in ((1, up_r), (2, up_l)):
-            cps.append(remote(wg.at[e], wgu.at[e, slot, :, 0:width], dev))
-            cps.append(remote(wu.at[e], wgu.at[e, slot, :, width:2 * width], dev))
-        return cps
+        if e < 2:
+            for cp in mine_gu[e]:
+                cp.wait()
+        return [remote(wgu.at[e, 0], wgu.at[e, slot], dev) for slot, dev in ((1, up_r), (2, up_l))]
 
     def pass_gu(e, cps):
         arrive(cps)
@@ -70,7 +82,8 @@
         ]
 
     def send_dn(n):
-        return [remote(wd.at[:, :, cols[n]], wdn[n].at[:, slot], dev) for slot, dev in ((1, up_r), (2, up_l))]
+        mine_dn[n].wait()
+        return [remote(wdn[n].at[:, 0], wdn[n].at[:, slot], dev) for slot, dev in ((1, up_r), (2, up_l))]
 
     def pass_dn(n, cps):
         arrive(cps)
@@ -79,25 +92,17 @@
             remote(wdn[n].at[he:n_e, 2], wdn[n].at[he:n_e, 3], up_l),
         ]
 
-    start = pl.multiple_of(q * rows, rows)
-    own_rows = hid.at[pl.ds(start, rows)]
-    route = [(a.at[:, pl.ds(start, rows)], v) for a, v in ((ids, ids_v), (gts, gts_v), (pos, pos_v))]
-
     def send_tok(dev):
-        return [remote(own_rows, tok.at[ep], dev)] + [remote(a, v.at[ep], dev) for a, v in route]
+        return [remote(tok.at[ep], tok.at[ep], dev)] + pass_route(ep, dev)
 
     def pass_route(b, dev):
         return [remote(v.at[b], v.at[b], dev) for v in (ids_v, gts_v, pos_v)]
 
     gu = {0: send_gu(0)}
-    tok_p, tok_r, tok_l = send_tok(to_p), send_tok(to_r), send_tok(to_l)
+    for cp in mine_tok:
+        cp.wait()
+    tok_r, tok_l, tok_p = send_tok(to_r), send_tok(to_l), send_tok(to_p)
     gu[1] = send_gu(1)
-    mine = [local(own_rows, tok.at[ep])] + [local(a, v.at[ep]) for a, v in route]
-    for e in range(n_e):
-        mine.append(local(wg.at[e], wgu.at[e, 0, :, 0:width]))
-        mine.append(local(wu.at[e], wgu.at[e, 0, :, width:2 * width]))
-    for n in range(n_c):
-        mine.append(local(wd.at[:, :, cols[n]], wdn[n].at[:, 0]))
 
     def block_at(o):
         h = lax.div(o, 2)
@@ -120,24 +125,28 @@
         lax.fori_loop(lo, hi, body, 0)
 
     def up(e0, e1, slots, lo, hi):
-        def body(t, carry):
-            b = block_at(lo + lax.div(t, e1 - e0))
-            e = e0 + lax.rem(t, e1 - e0)
-            gate = gcol[b, :, e0:e0 + 1] if e1 - e0 == 1 else None
-            if gate is None:
-                lane = lax.broadcasted_iota(jnp.int32, gcol.shape[1:], 1)
-                gate = jnp.sum(jnp.where(lane == e, gcol[b], 0.0), axis=1, keepdims=True)
-            for s in slots:
-                prod = jnp.dot(tok[b], wgu[e, s], preferred_element_type=jnp.float32)
-                h = jnp.where(gate > 0, jax.nn.silu(prod[:, :width]) * prod[:, width:], 0.0)
-                act[b * n_e + e, :, s * width:(s + 1) * width] = h.astype(jnp.bfloat16)
+        span = e1 - e0
+        total = (hi - lo) * span
+        step = max(span, 4 // len(slots))
+        while total % step:
+            step -= 1
+
+        def body(i, carry):
+            for k in range(step):
+                b, e = block_at(lo + i * (step // span) + k // span), e0 + k % span
+                gate = gcol[b, :, e:e + 1]
+                for s in slots:
+                    prod = jnp.dot(tok[b], wgu[e, s], preferred_element_type=jnp.float32)
+                    h = jnp.where(gate > 0, jax.nn.silu(prod[:, :width]) * prod[:, width:], 0.0)
+                    act[b * n_e + e, :, s * width:(s + 1) * width] = h.astype(jnp.bfloat16)
             return carry
 
-        lax.fori_loop(0, (hi - lo) * (e1 - e0), body, 0)
+        lax.fori_loop(0, total // step, body, 0)
 
     fwd, dn, fdn = {}, {}, {}
-    for cp in mine:
-        cp.wait()
+    for e in range(2, n_e):
+        for cp in mine_gu[e]:
+            cp.wait()
     arrive(tok_p)
     make_gates(0, 2)
     up(0, n_e, (0,), 0, 2)
@@ -197,6 +206,11 @@
         if n >= 1:
             d2d[n - 1].wait_send()
             sends[:] = [cp for cp in sends if cp is not d2d[n - 1]]
+        if n == n_c - 1:
+            drained = first[0] + second[0]
+            for cp in drained:
+                cp.wait_send()
+            sends[:] = [cp for cp in sends if not any(cp is old for old in drained)]
         half = spart.at[:, :, 0:wide[n]]
 
         def other(i, carry):
@@ -250,9 +264,9 @@
 
     def phase_d(n):
         arrive(second[n])
-        fin[n][...] = (acc[n][x] + r2[n][0] + r2[n][1]).astype(jnp.bfloat16)
-        outs[n] = [remote(fin[n], place(n, q, 0, rows), dev) for dev in (up_r, up_l)]
-        placed.append(local(fin[n], place(n, q, 0, rows)))
+        total = acc[n][x] + r2[n][0] + r2[n][1]
+        out[pl.ds(start, rows), cols[n]] = total.astype(jnp.bfloat16)
+        outs[n] = [remote(place(n, q, 0, rows), place(n, q, 0, rows), dev) for dev in (up_r, up_l)]
 
     def phase_e(n):
         arrive(outs[n])
@@ -299,8 +313,6 @@
         arrive(fouts[n])
     for cp in sends:
         cp.wait_send()
-    for cp in placed:
-        cp.wait()
 
 
 def solution(mesh):
@@ -319,15 +331,14 @@
         f32, bf16, i32 = jnp.float32, jnp.bfloat16, jnp.int32
         wide = [k * (d_model // 8) for k in EIGHTHS]
         chunked = [pltpu.VMEM((n_e, n_q, width, w), bf16) for w in wide]
-        chunked += [pltpu.VMEM((nx, rows, w), f32) for w in wide]
+        chunked += [pltpu.VMEM((nx, rows, w) if n < len(wide) - 1 else (8, 128), f32) for n, w in enumerate(wide)]
         chunked += [pltpu.VMEM((2, rows // 2, w), f32) for w in wide]
         chunked += [pltpu.VMEM((2, rows, w), f32) for w in wide]
-        chunked += [pltpu.VMEM((rows, w), bf16) for w in wide]
         return pl.pallas_call(
             functools.partial(moe_kernel, n_q, group),
-            out_shape=jax.ShapeDtypeStruct((rows_dev, d_model), bf16),
+            out_shape=pltpu.VMEM((rows_dev, d_model), bf16),
             in_specs=[pl.BlockSpec(memory_space=pl.ANY)] * 7,
-            out_specs=pl.BlockSpec(memory_space=pl.ANY),
+            out_specs=pl.BlockSpec(memory_space=pltpu.VMEM),
             scratch_shapes=[
                 pltpu.VMEM((group, rows, d_model), bf16),
                 pltpu.VMEM((group, top_k, rows), i32),
@@ -344,7 +355,7 @@
                 pltpu.SemaphoreType.DMA((24,)),
                 pltpu.SemaphoreType.REGULAR((2,)),
             ],
-            compiler_params=pltpu.CompilerParams(collective_id=0, has_side_effects=True, vmem_limit_bytes=67043328),
+            compiler_params=pltpu.CompilerParams(collective_id=0, has_side_effects=True, vmem_limit_bytes=59 * 1024 * 1024),
         )(hidden, expert_ids.T, gate_wts.T, slot_pos.T, w_gate, w_up, w_down)
 
     return jax.shard_map(device_step, mesh=mesh, in_specs=in_specs, out_specs=row_spec, check_vma=False)

time: 186 us -> 186 us (level); the launches traced: 186 us -> 183 us
  local copies, waits for them, and re-layouts: 4.64 us -> 2.02 us
    unnamed x1, local copies, waits for them, and re-layouts: 4.64 us -> 2.02 us
where the time goes in v4:
time: 186 us; the launch traced here: 183 us
  Pallas kernels  181 us (97%)
  local copies, waits for them, and re-layouts  2.02 us (1%)
    pallas_call x1, Pallas kernels, device_step(): pl.pallas_call(functools.partial(moe_kernel, n_q, group), out_shape=pltpu...  181 us

profile of v4, /device:TPU:97, one launch (start us, length us, event | category | flops | bytes accessed | tf_op | source)
XLA Modules:
  0.0 183.2 jit_solution(6886263706168270985)
XLA Ops:
  0.0 181.2 %shard_map.73 = bf16[2048,1024]{1,0:T(8,128)(2,1)S(1)} custom-call(bf16[2048,1024]{1,0:T(8,128)(2,1)} %hid.1, s32[8,2048]{1,0:T(8,128)} %bitcast.3, f32[8,2048]{1,0:T(8,128)} %bitcast.4, s32[8,2048]{1,0:T(8,128)} %bitcast.5, bf16[4,1024,128]{2,1,0:T(8,128)(2,1)} %wg.1, bf16[4,1024,128]{2,1,0:T(8,128)(2,1)} %wu.1, bf16[4,128,1024]{2,1,0:T(8,128)(2,1)} %wd.1), custom_call_target="tpu_custom_call" | custom-call | tf_op jit(solution)/shard_map/pallas_call | solution.py:337
  181.2 2.0 %copy.9 = bf16[2048,1024]{1,0:T(8,128)(2,1)} copy(bf16[2048,1024]{1,0:T(8,128)(2,1)S(1)} %shard_map.73) | data formatting | bytes 8388608

commit v5 on v4

--- a/solution.py
+++ b/solution.py
@@ -8,7 +8,7 @@
 from jax.sharding import PartitionSpec as P
 
 MESH = pl.DeviceIdType.MESH
-EIGHTHS = (1, 2, 2, 2, 1)
+EIGHTHS = (2, 2, 2, 1, 1)
 
 
 def moe_kernel(n_q, group, hid, ids, gts, pos, wg, wu, wd, out, tok, ids_v, gts_v, pos_v, gcol, wgu, act, spart, pr, *rest):
@@ -19,8 +19,8 @@
     n_e, width = wg.shape[0], wg.shape[2]
     nx = group // 2
     hr, hk, he = rows // 2, d_model // 2, n_e // 2
-    acc[n_c - 1] = acc[0]
     wide = [k * (d_model // 8) for k in EIGHTHS]
+    acc[n_c - 1] = acc[0].at[:, :, 0:wide[-1]]
     cols = [slice(sum(wide[:n]), sum(wide[:n + 1])) for n in range(n_c)]
     q, ep = lax.axis_index('etp'), lax.axis_index('ep')
     x, c = lax.div(ep, 2), lax.rem(ep, 2)
@@ -174,6 +174,7 @@
     arrive(fwd[0])
     up(0, 1, (3,), 0, 6)
     fwd[2] = pass_gu(2, gu[2])
+    dn[0] = send_dn(0)
     arrive(relay)
     make_gates(6, 8)
     up(0, n_e, (0,), 6, 8)
@@ -183,10 +184,11 @@
     arrive(fwd[1])
     up(1, 2, (3,), 0, 8)
     fwd[3] = pass_gu(3, gu[3])
-    dn[0] = send_dn(0)
     up(3, 4, (1, 2), 0, 8)
     arrive(fwd[2])
     up(2, 3, (3,), 0, 8)
+    fdn[0] = pass_dn(0, dn[0])
+    dn[1] = send_dn(1)
     arrive(fwd[3])
     up(3, 4, (3,), 0, 8)
 
@@ -199,55 +201,57 @@
             else:
                 dst[...] += term
 
-    d2d, first, second, outs, fouts = {}, {}, {}, {}, {}
-
-    def phase_a(n):
+    first, second, outs, fouts = {}, {}, {}, {}
+
+    d2d_base, used[0] = used[0], used[0] + nx * n_c
+
+    def to_partner(n, i):
+        xi, k = lax.rem(xf + i, nx), d2d_base + n * nx + i
+        return pltpu.make_async_remote_copy(
+            src_ref=spart.at[xi, :, 0:wide[n]], dst_ref=pr.at[n % 2, xi, :, 0:wide[n]],
+            send_sem=ssem.at[k], recv_sem=rsem.at[k], device_id=to_p, device_id_type=MESH)
+
+    def products(n, lo, hi):
+        def body(i, carry):
+            xi = lax.rem(xf + i, nx)
+            down(n, xi * 2 + 1 - c, spart.at[xi, :, 0:wide[n]])
+            to_partner(n, i).start()
+            down(n, xi * 2 + c, acc[n].at[xi])
+            return carry
+
+        lax.fori_loop(lo, hi, body, 0)
+
+    def join(n, i):
+        to_partner(n, i).wait_recv()
+        xi = lax.rem(xf + i, nx)
+        acc[n][xi] += pr[n % 2, xi, :, 0:wide[n]]
+
+    def phase_ab(n):
         arrive(fdn[n])
         if n >= 1:
-            d2d[n - 1].wait_send()
-            sends[:] = [cp for cp in sends if cp is not d2d[n - 1]]
+            for i in range(nx):
+                to_partner(n - 1, i).wait_send()
         if n == n_c - 1:
             drained = first[0] + second[0]
             for cp in drained:
                 cp.wait_send()
             sends[:] = [cp for cp in sends if not any(cp is old for old in drained)]
-        half = spart.at[:, :, 0:wide[n]]
-
-        def other(i, carry):
-            xi = lax.rem(xf + i, nx)
-            down(n, xi * 2 + 1 - c, half.at[xi])
-            return carry
-
-        lax.fori_loop(0, nx, other, 0)
         if n >= 2:
             pl.semaphore_wait(credit.at[n % 2], 1)
-        d2d[n] = remote(half, pr.at[n % 2, :, :, 0:wide[n]], to_p)
-
-        def own(i, carry):
-            xi = lax.rem(xf + i, nx)
-            down(n, xi * 2 + c, acc[n].at[xi])
-            return carry
-
-        lax.fori_loop(0, nx, own, 0)
-
-    def phase_b(n):
-        d2d[n].wait_recv()
-
-        def join(xi):
-            acc[n][xi] += pr[n % 2, xi, :, 0:wide[n]]
-
-        join(xf)
+        early = 2 if n == 0 else nx
+        products(n, 0, early)
+        join(n, 0)
         first[n] = [
             remote(acc[n].at[xf, 0:hr], r1[n].at[0], to_r),
             remote(acc[n].at[xf, hr:rows], r1[n].at[1], to_l),
         ]
-        join(xr)
-        join(xl)
-        second[n] = [
-            remote(acc[n].at[xr, hr:rows], r2[n].at[0, hr:rows], to_r),
-            remote(acc[n].at[xl, 0:hr], r2[n].at[1, 0:hr], to_l),
-        ]
-        join(x)
+        if early < nx:
+            products(n, early, nx)
+        join(n, 1)
+        second[n] = [remote(acc[n].at[xl, 0:hr], r2[n].at[1, 0:hr], to_l)]
+        join(n, 3)
+        second[n].append(remote(acc[n].at[xr, hr:rows], r2[n].at[0, hr:rows], to_r))
+        join(n, 2)
         if n + 2 < n_c:
             pl.semaphore_signal(credit.at[n % 2], inc=1, device_id=to_p, device_id_type=MESH)
 
@@ -266,40 +270,34 @@
         arrive(second[n])
         total = acc[n][x] + r2[n][0] + r2[n][1]
         out[pl.ds(start, rows), cols[n]] = total.astype(jnp.bfloat16)
-        outs[n] = [remote(place(n, q, 0, rows), place(n, q, 0, rows), dev) for dev in (up_r, up_l)]
+        low, high = place(n, q, 0, hr), place(n, q, hr, rows)
+        outs[n] = [remote(low, low, up_r), remote(high, high, up_l), remote(high, high, up_r), remote(low, low, up_l)]
 
     def phase_e(n):
-        arrive(outs[n])
+        arrive(outs[n][:2])
         fouts[n] = [
             remote(place(n, yl, 0, hr), place(n, yl, 0, hr), up_r),
             remote(place(n, yr, hr, rows), place(n, yr, hr, rows), up_l),
         ]
 
-    fdn[0] = pass_dn(0, dn[0])
-    dn[1] = send_dn(1)
+    phase_ab(0)
+    fdn[1] = pass_dn(1, dn[1])
     dn[2] = send_dn(2)
-    phase_a(0)
-    phase_b(0)
-    fdn[1] = pass_dn(1, dn[1])
+    phase_c(0)
+    phase_ab(1)
+    fdn[2] = pass_dn(2, dn[2])
     dn[3] = send_dn(3)
     dn[4] = send_dn(4)
-    phase_c(0)
-    phase_a(1)
-    phase_b(1)
-    fdn[2] = pass_dn(2, dn[2])
-    phase_a(2)
-    phase_b(2)
+    phase_ab(2)
     fdn[3] = pass_dn(3, dn[3])
     phase_c(1)
     phase_d(0)
-    phase_a(3)
-    phase_b(3)
+    phase_ab(3)
     fdn[4] = pass_dn(4, dn[4])
     phase_c(2)
     phase_d(1)
     phase_e(0)
-    phase_a(4)
-    phase_b(4)
+    phase_ab(4)
     phase_c(3)
     phase_d(2)
     phase_e(1)
@@ -309,8 +307,10 @@
     phase_d(4)
     phase_e(3)
     phase_e(4)
+    for i in range(nx):
+        to_partner(n_c - 1, i).wait_send()
     for n in range(n_c):
-        arrive(fouts[n])
+        arrive(outs[n][2:] + fouts[n])
     for cp in sends:
         cp.wait_send()
 
@@ -350,8 +350,8 @@
                 pltpu.VMEM((nx, rows, max(wide)), f32),
                 pltpu.VMEM((2, nx, rows, max(wide)), f32),
                 *chunked,
-                pltpu.SemaphoreType.DMA((132,)),
-                pltpu.SemaphoreType.DMA((132,)),
+                pltpu.SemaphoreType.DMA((152,)),
+                pltpu.SemaphoreType.DMA((152,)),
                 pltpu.SemaphoreType.DMA((24,)),
                 pltpu.SemaphoreType.REGULAR((2,)),
             ],

time: 186 us -> 174 us (0.935)
  Pallas kernels: 181 us -> 169 us
    pallas_call x1, Pallas kernels: 181 us -> 169 us  [device_step(): pl.pallas_call(functools.partial(moe_kernel, n_q, group), out_shape=pltpu...]
where the time goes in v5:
time: 174 us; the launch traced here: 171 us
  Pallas kernels  169 us (97%)
  local copies, waits for them, and re-layouts  2.02 us (1%)
    pallas_call x1, Pallas kernels, device_step(): pl.pallas_call(functools.partial(moe_kernel, n_q, group), out_shape=pltpu...  169 us

profile of v5, /device:TPU:97, one launch (start us, length us, event | category | flops | bytes accessed | tf_op | source)
XLA Modules:
  0.0 171.4 jit_solution(14248649210864118722)
XLA Ops:
  0.0 169.4 %shard_map.73 = bf16[2048,1024]{1,0:T(8,128)(2,1)S(1)} custom-call(bf16[2048,1024]{1,0:T(8,128)(2,1)} %hid.1, s32[8,2048]{1,0:T(8,128)} %bitcast.3, f32[8,2048]{1,0:T(8,128)} %bitcast.4, s32[8,2048]{1,0:T(8,128)} %bitcast.5, bf16[4,1024,128]{2,1,0:T(8,128)(2,1)} %wg.1, bf16[4,1024,128]{2,1,0:T(8,128)(2,1)} %wu.1, bf16[4,128,1024]{2,1,0:T(8,128)(2,1)} %wd.1), custom_call_target="tpu_custom_call" | custom-call | tf_op jit(solution)/shard_map/pallas_call | solution.py:337
  169.4 2.0 %copy.9 = bf16[2048,1024]{1,0:T(8,128)(2,1)} copy(bf16[2048,1024]{1,0:T(8,128)(2,1)S(1)} %shard_map.73) | data formatting | bytes 8388608

commit v6 on v5

--- a/solution.py
+++ b/solution.py
@@ -8,7 +8,7 @@
 from jax.sharding import PartitionSpec as P
 
 MESH = pl.DeviceIdType.MESH
-EIGHTHS = (2, 2, 2, 1, 1)
+EIGHTHS = (1, 1, 2, 2, 1, 1)
 
 
 def moe_kernel(n_q, group, hid, ids, gts, pos, wg, wu, wd, out, tok, ids_v, gts_v, pos_v, gcol, wgu, act, spart, pr, *rest):
@@ -20,7 +20,7 @@
     nx = group // 2
     hr, hk, he = rows // 2, d_model // 2, n_e // 2
     wide = [k * (d_model // 8) for k in EIGHTHS]
-    acc[n_c - 1] = acc[0].at[:, :, 0:wide[-1]]
+    acc[n_c - 2], acc[n_c - 1] = acc[0], acc[1]
     cols = [slice(sum(wide[:n]), sum(wide[:n + 1])) for n in range(n_c)]
     q, ep = lax.axis_index('etp'), lax.axis_index('ep')
     x, c = lax.div(ep, 2), lax.rem(ep, 2)
@@ -226,25 +226,27 @@
         xi = lax.rem(xf + i, nx)
         acc[n][xi] += pr[n % 2, xi, :, 0:wide[n]]
 
-    def phase_ab(n):
+    def phase_ab(n, hook=None):
         arrive(fdn[n])
         if n >= 1:
             for i in range(nx):
                 to_partner(n - 1, i).wait_send()
-        if n == n_c - 1:
-            drained = first[0] + second[0]
+        if n >= n_c - 2:
+            drained = first[n - n_c + 2] + second[n - n_c + 2]
             for cp in drained:
                 cp.wait_send()
             sends[:] = [cp for cp in sends if not any(cp is old for old in drained)]
         if n >= 2:
             pl.semaphore_wait(credit.at[n % 2], 1)
-        early = 2 if n == 0 else nx
+        early = 1 if n < 3 else nx
         products(n, 0, early)
         join(n, 0)
         first[n] = [
             remote(acc[n].at[xf, 0:hr], r1[n].at[0], to_r),
             remote(acc[n].at[xf, hr:rows], r1[n].at[1], to_l),
         ]
+        if hook is not None:
+            hook()
         if early < nx:
             products(n, early, nx)
         join(n, 1)
@@ -280,33 +282,37 @@
             remote(place(n, yr, hr, rows), place(n, yr, hr, rows), up_l),
         ]
 
-    phase_ab(0)
-    fdn[1] = pass_dn(1, dn[1])
-    dn[2] = send_dn(2)
-    phase_c(0)
-    phase_ab(1)
-    fdn[2] = pass_dn(2, dn[2])
-    dn[3] = send_dn(3)
-    dn[4] = send_dn(4)
-    phase_ab(2)
-    fdn[3] = pass_dn(3, dn[3])
+    def pass_on(n, *later):
+        fdn[n] = pass_dn(n, dn[n])
+        for k in later:
+            dn[k] = send_dn(k)
+
+    phase_ab(0, lambda: pass_on(1, 2))
+    phase_ab(1, lambda: phase_c(0))
+    pass_on(2, 3)
     phase_c(1)
-    phase_d(0)
+    phase_ab(2, lambda: phase_d(0))
+    pass_on(3, 4, 5)
+    phase_d(1)
+    phase_c(2)
     phase_ab(3)
-    fdn[4] = pass_dn(4, dn[4])
-    phase_c(2)
-    phase_d(1)
+    pass_on(4)
     phase_e(0)
+    phase_e(1)
     phase_ab(4)
+    pass_on(5)
+    phase_d(2)
     phase_c(3)
-    phase_d(2)
-    phase_e(1)
+    phase_ab(5)
+    phase_e(2)
     phase_c(4)
     phase_d(3)
-    phase_e(2)
+    phase_e(3)
+    phase_c(5)
     phase_d(4)
-    phase_e(3)
     phase_e(4)
+    phase_d(5)
+    phase_e(5)
     for i in range(nx):
         to_partner(n_c - 1, i).wait_send()
     for n in range(n_c):
@@ -331,7 +337,7 @@
         f32, bf16, i32 = jnp.float32, jnp.bfloat16, jnp.int32
         wide = [k * (d_model // 8) for k in EIGHTHS]
         chunked = [pltpu.VMEM((n_e, n_q, width, w), bf16) for w in wide]
-        chunked += [pltpu.VMEM((nx, rows, w) if n < len(wide) - 1 else (8, 128), f32) for n, w in enumerate(wide)]
+        chunked += [pltpu.VMEM((nx, rows, w) if n < len(wide) - 2 else (8, 128), f32) for n, w in enumerate(wide)]
         chunked += [pltpu.VMEM((2, rows // 2, w), f32) for w in wide]
         chunked += [pltpu.VMEM((2, rows, w), f32) for w in wide]
         return pl.pallas_call(
@@ -350,8 +356,8 @@
                 pltpu.VMEM((nx, rows, max(wide)), f32),
                 pltpu.VMEM((2, nx, rows, max(wide)), f32),
                 *chunked,
-                pltpu.SemaphoreType.DMA((152,)),
-                pltpu.SemaphoreType.DMA((152,)),
+                pltpu.SemaphoreType.DMA((168,)),
+                pltpu.SemaphoreType.DMA((168,)),
                 pltpu.SemaphoreType.DMA((24,)),
                 pltpu.SemaphoreType.REGULAR((2,)),
             ],

time: 174 us -> 174 us (level); the launches traced: 171 us -> 173 us
  Pallas kernels: 169 us -> 171 us
    pallas_call x1, Pallas kernels: 169 us -> 171 us  [device_step(): pl.pallas_call(functools.partial(moe_kernel, n_q, group), out_shape=pltpu...]
where the time goes in v6:
time: 174 us; the launch traced here: 173 us
  Pallas kernels  171 us (98%)
  local copies, waits for them, and re-layouts  2.02 us (1%)
    pallas_call x1, Pallas kernels, device_step(): pl.pallas_call(functools.partial(moe_kernel, n_q, group), out_shape=pltpu...  171 us

profile of v6, /device:TPU:97, one launch (start us, length us, event | category | flops | bytes accessed | tf_op | source)
XLA Modules:
  0.0 173.3 jit_solution(4234047675570529338)
XLA Ops:
  0.0 171.3 %shard_map.73 = bf16[2048,1024]{1,0:T(8,128)(2,1)S(1)} custom-call(bf16[2048,1024]{1,0:T(8,128)(2,1)} %hid.1, s32[8,2048]{1,0:T(8,128)} %bitcast.3, f32[8,2048]{1,0:T(8,128)} %bitcast.4, s32[8,2048]{1,0:T(8,128)} %bitcast.5, bf16[4,1024,128]{2,1,0:T(8,128)(2,1)} %wg.1, bf16[4,1024,128]{2,1,0:T(8,128)(2,1)} %wu.1, bf16[4,128,1024]{2,1,0:T(8,128)(2,1)} %wd.1), custom_call_target="tpu_custom_call" | custom-call | tf_op jit(solution)/shard_map/pallas_call | solution.py:343
  171.3 2.0 %copy.9 = bf16[2048,1024]{1,0:T(8,128)(2,1)} copy(bf16[2048,1024]{1,0:T(8,128)(2,1)S(1)} %shard_map.73) | data formatting | bytes 8388608

commit v7 on v5

--- a/solution.py
+++ b/solution.py
@@ -201,7 +201,8 @@
             else:
                 dst[...] += term
 
-    first, second, outs, fouts = {}, {}, {}, {}
+    first, second, late, outs, fouts = {}, {}, {}, {}, {}
+    parts = [1] * (n_c - 1) + [2]
 
     d2d_base, used[0] = used[0], used[0] + nx * n_c
 
@@ -232,7 +233,7 @@
             for i in range(nx):
                 to_partner(n - 1, i).wait_send()
         if n == n_c - 1:
-            drained = first[0] + second[0]
+            drained = first[0] + second[0] + sum(late[0], [])
             for cp in drained:
                 cp.wait_send()
             sends[:] = [cp for cp in sends if not any(cp is old for old in drained)]
@@ -258,26 +259,37 @@
     def phase_c(n):
         first[n][0].wait_recv()
         acc[n][xr, 0:hr] += r1[n][0]
-        second[n].append(remote(acc[n].at[xr, 0:hr], r2[n].at[0, 0:hr], to_r))
+        size = hr // parts[n]
+        late[n] = [[remote(acc[n].at[xr, p * size:(p + 1) * size], r2[n].at[0, p * size:(p + 1) * size], to_r)] for p in range(parts[n])]
         first[n][1].wait_recv()
         acc[n][xl, hr:rows] += r1[n][1]
-        second[n].append(remote(acc[n].at[xl, hr:rows], r2[n].at[1, hr:rows], to_l))
+        for p in range(parts[n]):
+            lo, hi = hr + p * size, hr + (p + 1) * size
+            late[n][p].append(remote(acc[n].at[xl, lo:hi], r2[n].at[1, lo:hi], to_l))
 
     def place(n, quarter, lo, hi):
-        return out.at[pl.ds(pl.multiple_of(quarter * rows + lo, hr), hi - lo), cols[n]]
-
-    def phase_d(n):
-        arrive(second[n])
-        total = acc[n][x] + r2[n][0] + r2[n][1]
-        out[pl.ds(start, rows), cols[n]] = total.astype(jnp.bfloat16)
-        low, high = place(n, q, 0, hr), place(n, q, hr, rows)
-        outs[n] = [remote(low, low, up_r), remote(high, high, up_l), remote(high, high, up_r), remote(low, low, up_l)]
-
-    def phase_e(n):
-        arrive(outs[n][:2])
-        fouts[n] = [
-            remote(place(n, yl, 0, hr), place(n, yl, 0, hr), up_r),
-            remote(place(n, yr, hr, rows), place(n, yr, hr, rows), up_l),
+        return out.at[pl.ds(pl.multiple_of(quarter * rows + lo, hr // 2), hi - lo), cols[n]]
+
+    def bands(n, p):
+        size = hr // parts[n]
+        return [(lo, lo + size) for lo in (p * size, hr + p * size)]
+
+    def phase_d(n, p=0):
+        if p == 0:
+            arrive(second[n])
+        arrive(late[n][p])
+        for lo, hi in bands(n, p):
+            total = acc[n][x, lo:hi] + r2[n][0, lo:hi] + r2[n][1, lo:hi]
+            out[pl.ds(pl.multiple_of(start + lo, hr // 2), hi - lo), cols[n]] = total.astype(jnp.bfloat16)
+        low, high = (place(n, q, lo, hi) for lo, hi in bands(n, p))
+        outs[n, p] = [remote(low, low, up_r), remote(high, high, up_l), remote(high, high, up_r), remote(low, low, up_l)]
+
+    def phase_e(n, p=0):
+        arrive(outs[n, p][:2])
+        (a, b), (c0, c1) = bands(n, p)
+        fouts[n, p] = [
+            remote(place(n, yl, a, b), place(n, yl, a, b), up_r),
+            remote(place(n, yr, c0, c1), place(n, yr, c0, c1), up_l),
         ]
 
     phase_ab(0)
@@ -306,11 +318,13 @@
     phase_e(2)
     phase_d(4)
     phase_e(3)
+    phase_d(4, 1)
     phase_e(4)
+    phase_e(4, 1)
     for i in range(nx):
         to_partner(n_c - 1, i).wait_send()
-    for n in range(n_c):
-        arrive(outs[n][2:] + fouts[n])
+    for key in sorted(outs):
+        arrive(outs[key][2:] + fouts[key])
     for cp in sends:
         cp.wait_send()
 
@@ -350,8 +364,8 @@
                 pltpu.VMEM((nx, rows, max(wide)), f32),
                 pltpu.VMEM((2, nx, rows, max(wide)), f32),
                 *chunked,
-                pltpu.SemaphoreType.DMA((152,)),
-                pltpu.SemaphoreType.DMA((152,)),
+                pltpu.SemaphoreType.DMA((164,)),
+                pltpu.SemaphoreType.DMA((164,)),
                 pltpu.SemaphoreType.DMA((24,)),
                 pltpu.SemaphoreType.REGULAR((2,)),
             ],

time: 174 us -> 175 us (level)
  no operation moved by 1% of the time
where the time goes in v7:
time: 175 us; the launch traced here: 172 us
  Pallas kernels  170 us (97%)
  local copies, waits for them, and re-layouts  2.02 us (1%)
    pallas_call x1, Pallas kernels, device_step(): pl.pallas_call(functools.partial(moe_kernel, n_q, group), out_shape=pltpu...  170 us

profile of v7, /device:TPU:97, one launch (start us, length us, event | category | flops | bytes accessed | tf_op | source)
XLA Modules:
  0.0 172.3 jit_solution(12534192046359404374)
XLA Ops:
  0.0 170.2 %shard_map.73 = bf16[2048,1024]{1,0:T(8,128)(2,1)S(1)} custom-call(bf16[2048,1024]{1,0:T(8,128)(2,1)} %hid.1, s32[8,2048]{1,0:T(8,128)} %bitcast.3, f32[8,2048]{1,0:T(8,128)} %bitcast.4, s32[8,2048]{1,0:T(8,128)} %bitcast.5, bf16[4,1024,128]{2,1,0:T(8,128)(2,1)} %wg.1, bf16[4,1024,128]{2,1,0:T(8,128)(2,1)} %wu.1, bf16[4,128,1024]{2,1,0:T(8,128)(2,1)} %wd.1), custom_call_target="tpu_custom_call" | custom-call | tf_op jit(solution)/shard_map/pallas_call | solution.py:351
  170.3 2.0 %copy.9 = bf16[2048,1024]{1,0:T(8,128)(2,1)} copy(bf16[2048,1024]{1,0:T(8,128)(2,1)S(1)} %shard_map.73) | data formatting | bytes 8388608
